TPU v7x, 32 devices: a whole 2x2x4 slice. The times are simulated.
32 devices in a mesh: member: 2 (over x), gx: 16 (over z, y, core).
Axes of the slice: x: 2, y: 2, z: 4, core: 2. Of those that a mesh axis runs over, the one named last changes fastest.
Arguments:
- spectrum: float32 [36, 32, 256, 128], P(None, None, ('member', 'gx')), parts along dimension 2, may hold values from 0 to 1
- wind: float32 [2, 256, 128], P(None, ('member', 'gx')), parts along dimension 1, may hold values from -32 to 32
- land_sea: int32 [128, 128], P('gx'), may hold values 0 or 1
- band_rows: int32 [128], replicated, may hold values from 0 to 127, each once
Outputs:
- spectrum_next: float32 [36, 32, 256, 128], P(None, None, ('member', 'gx')), parts along dimension 2
- ocean_fields: float32 [4, 128, 256], P(None, 'gx', 'member'), parts along dimension 2
There are 2 independent parts, one for each index of `member`. A program takes and returns all parts, laid end to end along the dimension named above; an argument that names none is the same for every part. Nothing has to cross between parts.
Inputs may be any that keep to these rules, and one draw needn't show every extreme that they name: band_rows names each of the 128 latitude rows exactly once.
All inputs are finite; a program needn't handle non-finite values. No bound on the sum of `land_sea` on one device may be relied on, other than what follows from the above.
Results may differ from a plain program's by a relative error of at most 0.00015.
Values sent between devices are 32-bit elements; how exact they have to be, the bound alone decides.
A program may use at most 128 MiB of HBM per device.

v0:
```python
import math
import jax
import jax.numpy as jnp
from jax import lax
from jax.sharding import PartitionSpec as P

STEPS = 3


def passed_along(value, axis, steps):
    count = lax.axis_size(axis)
    pairs = [(source, (source + steps) % count) for source in range(count)]
    return lax.ppermute(value, axis, pairs)


def wave_tables(directions, frequencies):
    angles = (jnp.arange(directions, dtype=jnp.float32) + 0.5) * (2.0 * math.pi / directions)
    levels = jnp.arange(frequencies, dtype=jnp.float32)
    shrink = jnp.power(jnp.float32(1.1), -levels)
    frequency = 0.0418 / shrink
    inverse_speed = 2.0 * math.pi * frequency / 9.81
    weight = (levels + 1.0) / frequencies
    cosine_dir = jnp.cos(angles)[:, None]
    sine_dir = jnp.sin(angles)[:, None]
    courant_x = 0.45 * shrink[None, :] * cosine_dir
    courant_y = 0.45 * shrink[None, :] * sine_dir
    factor = 3.0 / math.sqrt(directions * frequencies)
    project = jnp.stack(
        [factor * weight[None, :] * cosine_dir, factor * weight[None, :] * sine_dir]
    )
    return (courant_x, courant_y, cosine_dir, sine_dir, inverse_speed, weight * weight, project)


def upwind(center, west_cell, east_cell, courant_x, courant_y):
    along_x = courant_x[:, :, None, None]
    along_y = courant_y[:, :, None, None]
    border = jnp.zeros_like(center[..., :1])
    south_cell = jnp.concatenate([border, center[..., :-1]], axis=3)
    north_cell = jnp.concatenate([center[..., 1:], border], axis=3)
    return (
        center
        - jnp.maximum(along_x, 0.0) * (center - west_cell)
        + jnp.maximum(-along_x, 0.0) * (east_cell - center)
        - jnp.maximum(along_y, 0.0) * (center - south_cell)
        + jnp.maximum(-along_y, 0.0) * (north_cell - center)
    )


def sources(advected, wind_east, wind_north, sea_mask, tables):
    cosine_dir, sine_dir, inverse_speed, weight_two = (tables[2], tables[3], tables[4], tables[5])
    advected = advected * sea_mask
    energy = jnp.mean(advected, axis=(0, 1))
    wind_ratio = (
        wind_east * cosine_dir[:, :, None, None] + wind_north * sine_dir[:, :, None, None]
    ) * inverse_speed[None, :, None, None]
    growth = 0.05 * jnp.clip(wind_ratio - 1.0, 0.0, 4.0)
    damping = 0.3 * weight_two[None, :, None, None] * (energy / (0.5 + energy))
    return (advected * (1.0 + growth) / (1.0 + damping), growth * advected)


def coupling_fields(input_flux, current, project):
    stress = jnp.einsum("cij,ijxy->cxy", project, input_flux, precision=lax.Precision.HIGHEST)
    stokes = jnp.einsum("cij,ijxy->cxy", project, current, precision=lax.Precision.HIGHEST)
    return jnp.concatenate([stress, stokes], axis=0)


def per_device(spectrum, wind, land_sea, band_rows):
    tables = wave_tables(spectrum.shape[0], spectrum.shape[1])
    sea_mask = land_sea.astype(jnp.float32)
    current = spectrum
    quarter = spectrum.shape[0] // 4
    east_x = jnp.concatenate([tables[0][:quarter], tables[0][3 * quarter :]], axis=0)
    east_y = jnp.concatenate([tables[1][:quarter], tables[1][3 * quarter :]], axis=0)
    west_x = tables[0][quarter : 3 * quarter]
    west_y = tables[1][quarter : 3 * quarter]
    for step_index in range(STEPS):
        eastward = jnp.concatenate([current[:quarter], current[3 * quarter :]], axis=0)
        westward = current[quarter : 3 * quarter]
        from_west = passed_along(eastward[:, :, -1:], "gx", 1)
        from_east = passed_along(westward[:, :, :1], "gx", -1)
        west_cells = jnp.concatenate([from_west, eastward[:, :, :-1]], axis=2)
        east_cells = jnp.concatenate([westward[:, :, 1:], from_east], axis=2)
        moved_east = upwind(eastward, west_cells, eastward, east_x, east_y)
        moved_west = upwind(westward, westward, east_cells, west_x, west_y)
        advected = jnp.concatenate([moved_east[:quarter], moved_west, moved_east[quarter:]], axis=0)
        current, input_flux = sources(advected, wind[0], wind[1], sea_mask, tables)
    fields = coupling_fields(input_flux, current, tables[6])
    local_rows = jnp.transpose(fields[:, :, band_rows], (0, 2, 1))
    gathered = lax.all_gather(local_rows, "gx", axis=2, tiled=True)
    band_count = local_rows.shape[1] // lax.axis_size("gx")
    ocean_fields = lax.dynamic_slice_in_dim(
        gathered, lax.axis_index("gx") * band_count, band_count, 1
    )
    return (current, ocean_fields)


def solution(mesh):
    placed = (
        P(None, None, ("member", "gx"), None),
        P(None, ("member", "gx"), None),
        P("gx", None),
        P(),
    )
    return jax.shard_map(
        per_device,
        mesh=mesh,
        in_specs=placed,
        out_specs=(P(None, None, ("member", "gx"), None), P(None, "gx", "member")),
        check_vma=False,
    )
```

profile of v0, /device:TPU:0, one launch (start us, length us, event | category | flops | bytes accessed | tf_op | source)
XLA Modules:
  0.0 96.4 jit_solution(8376153678232764763)
XLA Ops:
  0.6 1.8 %fusion.60 = (f32[9,32,8,128]{3,2,1,0:T(8,128)S(1)}, f32[9,32,8,128]{3,2,1,0:T(8,128)S(1)}) fusion(f32[36,32,8,128]{3,2,1,0:T(8,128)} %param.4), kind=kLoop, calls=%fused_computation.121 | loop fusion | bytes 4718592 | tf_op jit(solution)/shard_map/slice | solution.py:77
  2.4 0.2 copy_dynamic-update-slice_fusion.1
  2.6 0.2 copy_dynamic-update-slice_fusion
  2.9 0.7 slice.228
  3.6 0.5 collective-permute-start
  4.1 0.8 copy-done
  4.9 0.2 slice.191
  5.1 5.5 %collective-permute-start.1 = (f32[18,32,1,128]{3,1,2,0:T(8,128)S(1)}, f32[18,32,1,128]{3,1,2,0:T(8,128)S(1)}, u32[]{:S(2)}, u32[]{:S(2)}) collective-permute-start(f32[18,32,1,128]{3,1,2,0:T(8,128)S(1)} %bitcast.18), channel_id=1, source_target_pairs={{0,15},{1,0},{2,1},{3,2},{4,3},{5,4},{6,5},{7,6},{8,7},{9,8},{10,9... | collective-permute-start | bytes 884744 | tf_op jit(solution)/shard_map/ppermute | solution.py:13
  10.6 3.1 %fusion.64 = (f32[18,32,8,127]{3,1,2,0:T(8,128)}, f32[18,32,8,127]{3,1,2,0:T(8,128)}) fusion(f32[18,32,8,128]{3,1,2,0:T(8,128)S(1)} %copy_dynamic-update-slice_fusion), kind=kLoop, calls=%fused_computation.125 | loop fusion | bytes 9363456 | tf_op jit(solution)/shard_map/slice | solution.py:38
  13.7 1.6 %slice.229 = f32[18,32,7,128]{3,1,2,0:T(8,128)} slice(f32[18,32,8,128]{3,1,2,0:T(8,128)S(1)} %copy_dynamic-update-slice_fusion), slice={[0:18], [0:32], [0:7], [0:128]} | slice | bytes 4128768 | tf_op jit(solution)/shard_map/slice | solution.py:81
  15.4 0.1 broadcast_multiply_fusion.1
  15.5 0.8 fusion.59
  16.3 0.2 slice.190
  16.6 1.8 %copy.58 = f32[18,32,8,127]{3,1,2,0:T(8,128)} copy(f32[18,32,8,127]{3,2,1,0:T(8,128)S(1)} %get-tuple-element.20) | data formatting | bytes 4681728
  18.5 1.9 %copy.59 = f32[18,32,8,127]{3,1,2,0:T(8,128)} copy(f32[18,32,8,127]{3,2,1,0:T(8,128)S(1)} %get-tuple-element.21) | data formatting | bytes 4681728
  20.3 1.7 %copy.56 = f32[18,32,7,128]{3,1,2,0:T(8,128)} copy(f32[18,32,7,128]{3,2,1,0:T(8,128)S(1)} %slice.190) | data formatting | bytes 4128768
  22.0 0.1 broadcast_multiply_fusion.3
  22.1 0.1 copy.41
  22.2 0.1 multiply_add_fusion
  22.4 4.0 %fusion.16 = f32[18,32,8,128]{3,1,2,0:T(8,128)S(1)} fusion(f32[18,32,8,128]{3,1,2,0:T(8,128)S(1)} %copy_dynamic-update-slice_fusion, f32[18,32,7,128]{3,1,2,0:T(8,128)} %slice.229, f32[18,32,1,128]{3,1,2,0:T(8,128)S(1)} %collective-permute-done, f32[18,32,8,127]{3,1,2,0:T(8,128)} %get-tuple-element.35, f32[18,32,8,127]{3,1,2,0:T(8,128)} %get-tuple-element.34, ...), kind=kLoop, calls=%fused_computation.43 | loop fusion | flops 7667712 | bytes 11768832 | tf_op jit(solution)/shard_map/add | solution.py:41
  26.4 0.3 fusion.63
  26.7 1.4 %slice-done = f32[18,32,8,128]{3,2,1,0:T(8,128)S(1)} async-done(((f32[36,32,8,128]{3,2,1,0:T(8,128)}), f32[18,32,8,128]{3,2,1,0:T(8,128)S(1)}, s32[]{:S(2)}) %slice-start) | async-done | bytes 2359320 | tf_op jit(solution)/shard_map/slice | solution.py:78
  28.1 0.7 copy-done.1
  28.8 1.7 %fusion.20 = f32[18,32,8,128]{3,1,2,0:T(8,128)S(1)} fusion(f32[18,32,1,128]{3,1,2,0:T(8,128)S(1)} %collective-permute-done.1, f32[18,32,7,128]{3,1,2,0:T(8,128)S(1)} %copy-done.3, f32[18,32,8,127]{3,1,2,0:T(8,128)S(1)} %copy-done.2, f32[18,32,8,127]{3,1,2,0:T(8,128)S(1)} %copy-done.1, f32[18,32,8,128]{3,2,1,0:T(8,128)S(1)} %slice-done, ...), kind=kLoop, calls=%fused_computation.48 | loop fusion | flops 7667712 | bytes 11768832 | tf_op jit(solution)/shard_map/add | solution.py:41
  30.6 0.6 fusion.7
  31.2 0.1 multiply_add_fusion.3
  31.2 1.4 %multiply_divide_fusion.2 = f32[36,32,8,128]{3,1,2,0:T(8,128)S(1)} fusion(f32[9,32,8,128]{3,1,2,0:T(8,128)S(1)} %get-tuple-element.33, f32[18,32,8,128]{3,1,2,0:T(8,128)S(1)} %fusion.20, f32[9,32,8,128]{3,1,2,0:T(8,128)S(1)} %get-tuple-element.32, f32[32,8,128]{2,0,1:T(8,128)S(1)} %multiply_add_fusion.3, f32[32]{0:T(128)S(1)} %power_multiply_fusion, ...), kind=kLoop, calls=%fused_computation.10 | loop fusion | flops 11796480 | bytes 9719936 | tf_op jit(solution)/shard_map/div | solution.py:58
  32.6 0.9 fusion.57
  33.5 0.3 fusion.58
  33.8 0.1 collective-permute-start.2
  33.9 0.2 fusion.40
  34.2 0.2 slice.250
  34.4 4.7 %collective-permute-start.3 = (f32[18,32,1,128]{3,1,2,0:T(8,128)S(1)}, f32[18,32,1,128]{3,1,2,0:T(8,128)S(1)}, u32[]{:S(2)}, u32[]{:S(2)}) collective-permute-start(f32[18,32,1,128]{3,1,2,0:T(8,128)S(1)} %slice.251), channel_id=1, source_target_pairs={{0,15},{1,0},{2,1},{3,2},{4,3},{5,4},{6,5},{7,6},{8,7},{9,8},{10,9... | collective-permute-start | bytes 884744 | tf_op jit(solution)/shard_map/ppermute | solution.py:13
  39.1 0.9 fusion.10
  39.9 2.8 %collective-permute-done.2 = f32[18,32,1,128]{3,1,2,0:T(8,128)S(1)} collective-permute-done((f32[18,32,1,128]{3,1,2,0:T(8,128)S(1)}, f32[18,32,1,128]{3,1,2,0:T(8,128)S(1)}, u32[]{:S(2)}, u32[]{:S(2)}) %collective-permute-start.2) | collective-permute-done | bytes 294944 | tf_op jit(solution)/shard_map/ppermute | solution.py:13
  42.7 1.9 %fusion.25 = f32[18,32,8,128]{3,1,2,0:T(8,128)S(1)} fusion(f32[18,32,7,128]{3,1,2,0:T(8,128)S(1)} %fusion.40, f32[18,32,1,128]{3,1,2,0:T(8,128)S(1)} %collective-permute-done.2, f32[18,32,8,127]{3,1,2,0:T(8,128)S(1)} %get-tuple-element.31, f32[18,32,8,127]{3,1,2,0:T(8,128)S(1)} %get-tuple-element.30, f32[9,32,8,128]{3,1,2,0:T(8,128)S(1)} %get-tuple-element.18, ...), kind=kLoop, calls=%fused_computation.54 | loop fusion | flops 8257536 | bytes 11768832 | tf_op jit(solution)/shard_map/add | solution.py:41
  44.7 0.2 fusion.62
  44.9 1.8 %fusion.29 = f32[18,32,8,128]{3,1,2,0:T(8,128)S(1)} fusion(f32[18,32,1,128]{3,1,2,0:T(8,128)S(1)} %collective-permute-done.3, f32[18,32,7,128]{3,1,2,0:T(8,128)S(1)} %slice.250, f32[18,32,8,127]{3,1,2,0:T(8,128)S(1)} %get-tuple-element.17, f32[18,32,8,127]{3,1,2,0:T(8,128)S(1)} %get-tuple-element.16, f32[36,32,8,128]{3,1,2,0:T(8,128)S(1)} %multiply_divide_fusion.2, ...), kind=kLoop, calls=%fused_computation.59 | loop fusion | flops 7667712 | bytes 11768832 | tf_op jit(solution)/shard_map/add | solution.py:41
  46.7 0.6 fusion.6
  47.3 0.1 multiply_add_fusion.2
  47.4 1.4 %multiply_divide_fusion.1 = f32[36,32,8,128]{3,1,2,0:T(8,128)S(1)} fusion(f32[9,32,8,128]{3,1,2,0:T(8,128)S(1)} %get-tuple-element.29, f32[18,32,8,128]{3,1,2,0:T(8,128)S(1)} %fusion.29, f32[9,32,8,128]{3,1,2,0:T(8,128)S(1)} %get-tuple-element.28, f32[32,8,128]{2,0,1:T(8,128)S(1)} %multiply_add_fusion.2, f32[32]{0:T(128)S(1)} %power_multiply_fusion, ...), kind=kLoop, calls=%fused_computation.9 | loop fusion | flops 11796480 | bytes 9719936 | tf_op jit(solution)/shard_map/div | solution.py:58
  48.8 0.9 fusion.55
  49.6 0.3 fusion.56
  50.0 0.1 collective-permute-start.4
  50.0 0.2 fusion.39
  50.3 0.2 slice.267
  50.5 4.5 %collective-permute-start.5 = (f32[18,32,1,128]{3,1,2,0:T(8,128)S(1)}, f32[18,32,1,128]{3,1,2,0:T(8,128)S(1)}, u32[]{:S(2)}, u32[]{:S(2)}) collective-permute-start(f32[18,32,1,128]{3,1,2,0:T(8,128)S(1)} %slice.268), channel_id=1, source_target_pairs={{0,15},{1,0},{2,1},{3,2},{4,3},{5,4},{6,5},{7,6},{8,7},{9,8},{10,9... | collective-permute-start | bytes 884744 | tf_op jit(solution)/shard_map/ppermute | solution.py:13
  55.0 0.9 fusion.8
  55.9 3.0 %collective-permute-done.4 = f32[18,32,1,128]{3,1,2,0:T(8,128)S(1)} collective-permute-done((f32[18,32,1,128]{3,1,2,0:T(8,128)S(1)}, f32[18,32,1,128]{3,1,2,0:T(8,128)S(1)}, u32[]{:S(2)}, u32[]{:S(2)}) %collective-permute-start.4) | collective-permute-done | bytes 294944 | tf_op jit(solution)/shard_map/ppermute | solution.py:13
  58.9 1.9 %fusion.34 = f32[18,32,8,128]{3,1,2,0:T(8,128)S(1)} fusion(f32[18,32,7,128]{3,1,2,0:T(8,128)S(1)} %fusion.39, f32[18,32,1,128]{3,1,2,0:T(8,128)S(1)} %collective-permute-done.4, f32[18,32,8,127]{3,1,2,0:T(8,128)S(1)} %get-tuple-element.27, f32[18,32,8,127]{3,1,2,0:T(8,128)S(1)} %get-tuple-element.26, f32[9,32,8,128]{3,1,2,0:T(8,128)S(1)} %get-tuple-element.14, ...), kind=kLoop, calls=%fused_computation.65 | loop fusion | flops 8257536 | bytes 11768832 | tf_op jit(solution)/shard_map/add | solution.py:41
  60.8 0.2 fusion.61
  61.0 1.8 %fusion.38 = f32[18,32,8,128]{3,1,2,0:T(8,128)S(1)} fusion(f32[18,32,1,128]{3,1,2,0:T(8,128)S(1)} %collective-permute-done.5, f32[18,32,7,128]{3,1,2,0:T(8,128)S(1)} %slice.267, f32[18,32,8,127]{3,1,2,0:T(8,128)S(1)} %get-tuple-element.13, f32[18,32,8,127]{3,1,2,0:T(8,128)S(1)} %get-tuple-element.12, f32[36,32,8,128]{3,1,2,0:T(8,128)S(1)} %multiply_divide_fusion.1, ...), kind=kLoop, calls=%fused_computation.70 | loop fusion | flops 7667712 | bytes 11768832 | tf_op jit(solution)/shard_map/add | solution.py:41
  62.8 0.6 fusion.41
  63.4 0.1 multiply_add_fusion.1
  63.5 1.8 %fusion.4 = (f32[36,32,8,128]{3,1,2,0:T(8,128)S(1)}, f32[36,32,8,128]{3,1,2,0:T(8,128)S(1)}) fusion(f32[32]{0:T(128)S(1)} %power_multiply_fusion, f32[36,8,128]{2,1,0:T(8,128)S(1)} %multiply_add_fusion, f32[8,128]{1,0:T(8,128)S(1)} %convert_element_type.3, f32[9,32,8,128]{3,1,2,0:T(8,128)S(1)} %get-tuple-element.25, f32[18,32,8,128]{3,1,2,0:T(8,128)S(1)} %fusion.38, ...), kind=kLoop, calls=%fused_computation.12 | loop fusion | flops 12976128 | bytes 14438528 | tf_op jit(solution)/shard_map/mul | solution.py:58
  65.3 6.5 %copy.39 = f32[36,32,8,128]{3,2,1,0:T(8,128)} copy(f32[36,32,8,128]{3,1,2,0:T(8,128)S(1)} %get-tuple-element.11) | data formatting | bytes 9437184
  71.8 2.4 %fusion.45 = f32[2,8,128]{2,0,1:T(2,128)S(1)} fusion(f32[2,36,32,1]{2,0,1,3:T(2,128)S(1)} %copy.41, f32[36,32,8,128]{3,1,2,0:T(8,128)S(1)} %get-tuple-element.11), kind=kOutput, calls=%fused_computation.77 | convolution fusion | flops 28311552 | bytes 4736000 | tf_op jit(solution)/shard_map/cij,ijxy->cxy/dot_general | solution.py:63
  74.2 2.4 %fusion.42 = f32[2,8,128]{2,0,1:T(2,128)S(1)} fusion(f32[2,36,32,1]{2,0,1,3:T(2,128)S(1)} %copy.41, f32[36,32,8,128]{3,1,2,0:T(8,128)S(1)} %get-tuple-element.10), kind=kOutput, calls=%fused_computation.76 | convolution fusion | flops 28311552 | bytes 4736000 | tf_op jit(solution)/shard_map/cij,ijxy->cxy/dot_general | solution.py:62
  76.6 0.2 copy.37
  76.8 0.8 gather_fusion
  77.5 0.1 copy.38
  77.6 17.9 %all_gather.3 = f32[4,128,128]{1,0,2:T(4,128)S(1)} all-gather(f32[4,128,8]{1,0,2:T(4,128)S(1)} %copy.38), channel_id=1, replica_groups=mesh['member'=2,'gx'=16] {'gx'}, dimensions={2}, use_global_device_ids=true | all-gather | bytes 278528 | tf_op jit(solution)/shard_map/all_gather | solution.py:89
  95.5 0.2 constant_dynamic-slice_fusion
  95.7 0.7 copy.40
  (41 shorter events, 0.3 us)
Async XLA Ops:
  2.4 2.4 %copy-start = (f32[36,32,8,128]{3,2,1,0:T(8,128)S(1)}, f32[36,32,8,128]{3,2,1,0:T(8,128)}, u32[]{:S(2)}) copy-start(f32[36,32,8,128]{3,2,1,0:T(8,128)} %param.4) | copy-start | bytes 14155780
  3.6 18.8 %collective-permute-start = (f32[18,32,1,128]{3,1,2,0:T(8,128)}, f32[18,32,1,128]{3,1,2,0:T(8,128)S(1)}, u32[]{:S(2)}, u32[]{:S(2)}) collective-permute-start(f32[18,32,1,128]{3,1,2,0:T(8,128)} %slice.228), channel_id=1, source_target_pairs={{0,1},{1,2},{2,3},{3,4},{4,5},{5,6},{6,7},{7,8},{8,9},{9,10},{10,1... | collective-permute-start | bytes 884744 | tf_op jit(solution)/shard_map/ppermute | solution.py:13
  5.1 21.7 %collective-permute-start.1 = (f32[18,32,1,128]{3,1,2,0:T(8,128)S(1)}, f32[18,32,1,128]{3,1,2,0:T(8,128)S(1)}, u32[]{:S(2)}, u32[]{:S(2)}) collective-permute-start(f32[18,32,1,128]{3,1,2,0:T(8,128)S(1)} %bitcast.18), channel_id=1, source_target_pairs={{0,15},{1,0},{2,1},{3,2},{4,3},{5,4},{6,5},{7,6},{8,7},{9,8},{10,9... | collective-permute-start | bytes 884744 | tf_op jit(solution)/shard_map/ppermute | solution.py:13
  20.3 1.7 %copy-start.5 = (s32[8,128]{1,0:T(8,128)S(1)}, s32[8,128]{1,0:T(8,128)}, u32[]{:S(2)}) copy-start(s32[8,128]{1,0:T(8,128)} %param.6) | copy-start | bytes 12292
  20.3 1.7 %copy-start.4 = (f32[2,8,128]{2,1,0:T(8,128)S(1)}, f32[2,8,128]{2,1,0:T(8,128)}, u32[]{:S(2)}) copy-start(f32[2,8,128]{2,1,0:T(8,128)} %param.5) | copy-start | bytes 24580
  20.3 1.9 %copy-start.6 = (s32[128]{0:T(128)S(1)}, s32[128]{0:T(128)}, u32[]{:S(2)}) copy-start(s32[128]{0:T(128)} %param.7) | copy-start | bytes 1540
  22.4 4.3 %copy-start.2 = (f32[18,32,8,127]{3,1,2,0:T(8,128)S(1)}, f32[18,32,8,127]{3,1,2,0:T(8,128)}, u32[]{:S(2)}) copy-start(f32[18,32,8,127]{3,1,2,0:T(8,128)} %copy.59) | copy-start | bytes 7022596
  22.4 4.3 %copy-start.3 = (f32[18,32,7,128]{3,1,2,0:T(8,128)S(1)}, f32[18,32,7,128]{3,1,2,0:T(8,128)}, u32[]{:S(2)}) copy-start(f32[18,32,7,128]{3,1,2,0:T(8,128)} %copy.56) | copy-start | bytes 6193156
  26.4 1.7 %slice-start = ((f32[36,32,8,128]{3,2,1,0:T(8,128)}), f32[18,32,8,128]{3,2,1,0:T(8,128)S(1)}, s32[]{:S(2)}) async-start(f32[36,32,8,128]{3,2,1,0:T(8,128)} %param.4), calls=%async_computation | async-start | bytes 4718592 | tf_op jit(solution)/shard_map/slice | solution.py:78
  26.4 2.4 %copy-start.1 = (f32[18,32,8,127]{3,1,2,0:T(8,128)S(1)}, f32[18,32,8,127]{3,1,2,0:T(8,128)}, u32[]{:S(2)}) copy-start(f32[18,32,8,127]{3,1,2,0:T(8,128)} %copy.58) | copy-start | bytes 7022596
  33.8 8.9 %collective-permute-start.2 = (f32[18,32,1,128]{3,1,2,0:T(8,128)S(1)}, f32[18,32,1,128]{3,1,2,0:T(8,128)S(1)}, u32[]{:S(2)}, u32[]{:S(2)}) collective-permute-start(f32[18,32,1,128]{3,1,2,0:T(8,128)S(1)} %fusion.49), channel_id=1, source_target_pairs={{0,1},{1,2},{2,3},{3,4},{4,5},{5,6},{6,7},{7,8},{8,9},{9,10},{10,1... | collective-permute-start | bytes 884744 | tf_op jit(solution)/shard_map/ppermute | solution.py:13
  34.4 10.5 %collective-permute-start.3 = (f32[18,32,1,128]{3,1,2,0:T(8,128)S(1)}, f32[18,32,1,128]{3,1,2,0:T(8,128)S(1)}, u32[]{:S(2)}, u32[]{:S(2)}) collective-permute-start(f32[18,32,1,128]{3,1,2,0:T(8,128)S(1)} %slice.251), channel_id=1, source_target_pairs={{0,15},{1,0},{2,1},{3,2},{4,3},{5,4},{6,5},{7,6},{8,7},{9,8},{10,9... | collective-permute-start | bytes 884744 | tf_op jit(solution)/shard_map/ppermute | solution.py:13
  50.0 8.9 %collective-permute-start.4 = (f32[18,32,1,128]{3,1,2,0:T(8,128)S(1)}, f32[18,32,1,128]{3,1,2,0:T(8,128)S(1)}, u32[]{:S(2)}, u32[]{:S(2)}) collective-permute-start(f32[18,32,1,128]{3,1,2,0:T(8,128)S(1)} %fusion.48), channel_id=1, source_target_pairs={{0,1},{1,2},{2,3},{3,4},{4,5},{5,6},{6,7},{7,8},{8,9},{9,10},{10,1... | collective-permute-start | bytes 884744 | tf_op jit(solution)/shard_map/ppermute | solution.py:13
  50.5 10.5 %collective-permute-start.5 = (f32[18,32,1,128]{3,1,2,0:T(8,128)S(1)}, f32[18,32,1,128]{3,1,2,0:T(8,128)S(1)}, u32[]{:S(2)}, u32[]{:S(2)}) collective-permute-start(f32[18,32,1,128]{3,1,2,0:T(8,128)S(1)} %slice.268), channel_id=1, source_target_pairs={{0,15},{1,0},{2,1},{3,2},{4,3},{5,4},{6,5},{7,6},{8,7},{9,8},{10,9... | collective-permute-start | bytes 884744 | tf_op jit(solution)/shard_map/ppermute | solution.py:13
where the time goes:
time: 96.6 us; the launch traced here: 96.4 us
  local copies, waits for them, and re-layouts  29.2 us (30%)
  other arithmetic  22.3 us (23%)
  blocking collectives  17.9 us (19%)
  starting transfers between devices  15.3 us (16%)
  waiting for transfers between devices  5.77 us (6%)
  matrix products  4.79 us (5%)
  between operations  1.14 us (1%)
    all_gather x1, blocking collectives, per_device(): gathered = lax.all_gather(local_rows, 'gx', axis=2, tiled=True)  17.9 us
    ppermute x6, starting transfers between devices, passed_along(): return lax.ppermute(value, axis, pairs)  15.3 us
    unnamed x20, local copies, waits for them, and re-layouts  14.3 us
    add x6, other arithmetic, upwind(): center - jnp.maximum(along_x, 0.0) * (center - west_cell)  13.1 us
    ppermute x6, waiting for transfers between devices, passed_along(): return lax.ppermute(value, axis, pairs)  5.77 us
    slice x4, local copies, waits for them, and re-layouts, upwind(): south_cell = jnp.concatenate([border, center[..., :-1]], axis=3)  5.63 us
    div x2, other arithmetic, sources(): return (advected * (1.0 + growth) / (1.0 + damping), growth * advected)  2.77 us
    dot_general x1, matrix products, coupling_fields(): jnp.einsum('cij,ijxy->cxy', project, input_flux, precision=lax.Precision....  2.41 us
  transfers between devices with their start and end apart: 6, of which 2 were waited for; matrix products, arithmetic and copies ran while one was open for 24% of the time, Pallas kernels for 0%

commit v1 on v0

--- a/solution.py
+++ b/solution.py
@@ -86,7 +86,9 @@
         current, input_flux = sources(advected, wind[0], wind[1], sea_mask, tables)
     fields = coupling_fields(input_flux, current, tables[6])
     local_rows = jnp.transpose(fields[:, :, band_rows], (0, 2, 1))
-    gathered = lax.all_gather(local_rows, "gx", axis=2, tiled=True)
+    gathered = jnp.concatenate(
+        lax.all_to_all(jnp.stack([local_rows] * lax.axis_size("gx")), "gx", 0, 0), axis=2
+    )
     band_count = local_rows.shape[1] // lax.axis_size("gx")
     ocean_fields = lax.dynamic_slice_in_dim(
         gathered, lax.axis_index("gx") * band_count, band_count, 1

time: 96.6 us -> 87.3 us (0.904)
  blocking collectives: 17.9 us -> 0 us
  starting transfers between devices: 15.3 us -> 19.9 us
  local copies, waits for them, and re-layouts: 29.2 us -> 32.3 us
    all_gather x1 -> x0, blocking collectives: 17.9 us -> none  [per_device(): gathered = lax.all_gather(local_rows, 'gx', axis=2, tiled=True)]
    all_to_all x0 -> x1, starting transfers between devices: none -> 4.44 us  [per_device(): lax.all_to_all(jnp.stack([local_rows] * lax.axis_size('gx')), 'gx', 0, 0)]
    unnamed x20 -> x22, local copies, waits for them, and re-layouts: 14.3 us -> 16.6 us
    all_to_all x0 -> x1, waiting for transfers between devices: none -> 1.15 us  [per_device(): lax.all_to_all(jnp.stack([local_rows] * lax.axis_size('gx')), 'gx', 0, 0)]
  transfers between devices with their start and end apart: 6 -> 7, of which waited for: 2 -> 3; matrix products, arithmetic and copies ran while one was open for 24% -> 37% of each run, Pallas kernels for 0% -> 0%
where the time goes in v1:
time: 87.3 us; the launch traced here: 87 us
  local copies, waits for them, and re-layouts  32.3 us (37%)
  other arithmetic  22.1 us (25%)
  starting transfers between devices  19.9 us (23%)
  waiting for transfers between devices  6.7 us (8%)
  matrix products  4.8 us (5%)
  between operations  1.16 us (1%)
    unnamed x22, local copies, waits for them, and re-layouts  16.6 us
    ppermute x6, starting transfers between devices, passed_along(): return lax.ppermute(value, axis, pairs)  15.5 us
    add x6, other arithmetic, upwind(): center - jnp.maximum(along_x, 0.0) * (center - west_cell)  13.1 us
    slice x4, local copies, waits for them, and re-layouts, upwind(): south_cell = jnp.concatenate([border, center[..., :-1]], axis=3)  5.63 us
    ppermute x6, waiting for transfers between devices, passed_along(): return lax.ppermute(value, axis, pairs)  5.55 us
    all_to_all x1, starting transfers between devices, per_device(): lax.all_to_all(jnp.stack([local_rows] * lax.axis_size('gx')), 'gx', 0, 0)  4.44 us
    div x2, other arithmetic, sources(): return (advected * (1.0 + growth) / (1.0 + damping), growth * advected)  2.77 us
    dot_general x1, matrix products, coupling_fields(): jnp.einsum('cij,ijxy->cxy', project, input_flux, precision=lax.Precision....  2.4 us
  transfers between devices with their start and end apart: 7, of which 3 were waited for; matrix products, arithmetic and copies ran while one was open for 37% of the time, Pallas kernels for 0%

profile of v1, /device:TPU:0, one launch (start us, length us, event | category | flops | bytes accessed | tf_op | source)
XLA Modules:
  0.0 87.0 jit_solution(1249808869936672601)
XLA Ops:
  0.6 1.8 %fusion.60 = (f32[9,32,8,128]{3,2,1,0:T(8,128)S(1)}, f32[9,32,8,128]{3,2,1,0:T(8,128)S(1)}) fusion(f32[36,32,8,128]{3,2,1,0:T(8,128)} %param.4), kind=kLoop, calls=%fused_computation.122 | loop fusion | bytes 4718592 | tf_op jit(solution)/shard_map/slice | solution.py:77
  2.4 0.2 copy_dynamic-update-slice_fusion.1
  2.6 0.2 copy_dynamic-update-slice_fusion
  2.9 0.7 slice.228
  3.6 0.5 collective-permute-start
  4.1 0.8 copy-done.1
  4.9 0.2 slice.191
  5.1 5.5 %collective-permute-start.1 = (f32[18,32,1,128]{3,1,2,0:T(8,128)S(1)}, f32[18,32,1,128]{3,1,2,0:T(8,128)S(1)}, u32[]{:S(2)}, u32[]{:S(2)}) collective-permute-start(f32[18,32,1,128]{3,1,2,0:T(8,128)S(1)} %bitcast.24), channel_id=1, source_target_pairs={{0,15},{1,0},{2,1},{3,2},{4,3},{5,4},{6,5},{7,6},{8,7},{9,8},{10,9... | collective-permute-start | bytes 884744 | tf_op jit(solution)/shard_map/ppermute | solution.py:13
  10.6 3.1 %fusion.64 = (f32[18,32,8,127]{3,1,2,0:T(8,128)}, f32[18,32,8,127]{3,1,2,0:T(8,128)}) fusion(f32[18,32,8,128]{3,1,2,0:T(8,128)S(1)} %copy_dynamic-update-slice_fusion), kind=kLoop, calls=%fused_computation.126 | loop fusion | bytes 9363456 | tf_op jit(solution)/shard_map/slice | solution.py:38
  13.7 1.6 %slice.229 = f32[18,32,7,128]{3,1,2,0:T(8,128)} slice(f32[18,32,8,128]{3,1,2,0:T(8,128)S(1)} %copy_dynamic-update-slice_fusion), slice={[0:18], [0:32], [0:7], [0:128]} | slice | bytes 4128768 | tf_op jit(solution)/shard_map/slice | solution.py:81
  15.4 0.1 broadcast_multiply_fusion.1
  15.5 0.8 fusion.59
  16.3 0.2 slice.190
  16.6 1.8 %copy.61 = f32[18,32,8,127]{3,1,2,0:T(8,128)} copy(f32[18,32,8,127]{3,2,1,0:T(8,128)S(1)} %get-tuple-element.18) | data formatting | bytes 4681728
  18.4 1.9 %copy.62 = f32[18,32,8,127]{3,1,2,0:T(8,128)} copy(f32[18,32,8,127]{3,2,1,0:T(8,128)S(1)} %get-tuple-element.19) | data formatting | bytes 4681728
  20.3 1.7 %copy.59 = f32[18,32,7,128]{3,1,2,0:T(8,128)} copy(f32[18,32,7,128]{3,2,1,0:T(8,128)S(1)} %slice.190) | data formatting | bytes 4128768
  22.0 0.1 broadcast_multiply_fusion.3
  22.1 0.1 copy.44
  22.2 0.1 multiply_add_fusion
  22.4 4.0 %fusion.16 = f32[18,32,8,128]{3,1,2,0:T(8,128)S(1)} fusion(f32[18,32,8,128]{3,1,2,0:T(8,128)S(1)} %copy_dynamic-update-slice_fusion, f32[18,32,7,128]{3,1,2,0:T(8,128)} %slice.229, f32[18,32,1,128]{3,1,2,0:T(8,128)S(1)} %collective-permute-done, f32[18,32,8,127]{3,1,2,0:T(8,128)} %get-tuple-element.33, f32[18,32,8,127]{3,1,2,0:T(8,128)} %get-tuple-element.32, ...), kind=kLoop, calls=%fused_computation.43 | loop fusion | flops 7667712 | bytes 11768832 | tf_op jit(solution)/shard_map/add | solution.py:41
  26.4 0.3 fusion.63
  26.7 1.4 %slice-done = f32[18,32,8,128]{3,2,1,0:T(8,128)S(1)} async-done(((f32[36,32,8,128]{3,2,1,0:T(8,128)}), f32[18,32,8,128]{3,2,1,0:T(8,128)S(1)}, s32[]{:S(2)}) %slice-start) | async-done | bytes 2359320 | tf_op jit(solution)/shard_map/slice | solution.py:78
  28.1 0.7 copy-done.2
  28.8 1.7 %fusion.20 = f32[18,32,8,128]{3,1,2,0:T(8,128)S(1)} fusion(f32[18,32,1,128]{3,1,2,0:T(8,128)S(1)} %collective-permute-done.1, f32[18,32,7,128]{3,1,2,0:T(8,128)S(1)} %copy-done.4, f32[18,32,8,127]{3,1,2,0:T(8,128)S(1)} %copy-done.3, f32[18,32,8,127]{3,1,2,0:T(8,128)S(1)} %copy-done.2, f32[18,32,8,128]{3,2,1,0:T(8,128)S(1)} %slice-done, ...), kind=kLoop, calls=%fused_computation.48 | loop fusion | flops 7667712 | bytes 11768832 | tf_op jit(solution)/shard_map/add | solution.py:41
  30.5 0.6 fusion.7
  31.1 0.1 multiply_add_fusion.3
  31.2 1.4 %multiply_divide_fusion.2 = f32[36,32,8,128]{3,1,2,0:T(8,128)S(1)} fusion(f32[9,32,8,128]{3,1,2,0:T(8,128)S(1)} %get-tuple-element.31, f32[18,32,8,128]{3,1,2,0:T(8,128)S(1)} %fusion.20, f32[9,32,8,128]{3,1,2,0:T(8,128)S(1)} %get-tuple-element.30, f32[32,8,128]{2,0,1:T(8,128)S(1)} %multiply_add_fusion.3, f32[32]{0:T(128)S(1)} %power_multiply_fusion, ...), kind=kLoop, calls=%fused_computation.10 | loop fusion | flops 11796480 | bytes 9719936 | tf_op jit(solution)/shard_map/div | solution.py:58
  32.6 0.9 fusion.57
  33.5 0.3 fusion.58
  33.9 0.2 fusion.40
  34.1 0.2 slice.250
  34.4 4.7 %collective-permute-start.3 = (f32[18,32,1,128]{3,1,2,0:T(8,128)S(1)}, f32[18,32,1,128]{3,1,2,0:T(8,128)S(1)}, u32[]{:S(2)}, u32[]{:S(2)}) collective-permute-start(f32[18,32,1,128]{3,1,2,0:T(8,128)S(1)} %slice.251), channel_id=1, source_target_pairs={{0,15},{1,0},{2,1},{3,2},{4,3},{5,4},{6,5},{7,6},{8,7},{9,8},{10,9... | collective-permute-start | bytes 884744 | tf_op jit(solution)/shard_map/ppermute | solution.py:13
  39.1 0.9 fusion.10
  39.9 2.8 %collective-permute-done.2 = f32[18,32,1,128]{3,1,2,0:T(8,128)S(1)} collective-permute-done((f32[18,32,1,128]{3,1,2,0:T(8,128)S(1)}, f32[18,32,1,128]{3,1,2,0:T(8,128)S(1)}, u32[]{:S(2)}, u32[]{:S(2)}) %collective-permute-start.2) | collective-permute-done | bytes 294944 | tf_op jit(solution)/shard_map/ppermute | solution.py:13
  42.7 1.9 %fusion.25 = f32[18,32,8,128]{3,1,2,0:T(8,128)S(1)} fusion(f32[18,32,7,128]{3,1,2,0:T(8,128)S(1)} %fusion.40, f32[18,32,1,128]{3,1,2,0:T(8,128)S(1)} %collective-permute-done.2, f32[18,32,8,127]{3,1,2,0:T(8,128)S(1)} %get-tuple-element.29, f32[18,32,8,127]{3,1,2,0:T(8,128)S(1)} %get-tuple-element.28, f32[9,32,8,128]{3,1,2,0:T(8,128)S(1)} %get-tuple-element.16, ...), kind=kLoop, calls=%fused_computation.54 | loop fusion | flops 8257536 | bytes 11768832 | tf_op jit(solution)/shard_map/add | solution.py:41
  44.6 0.2 fusion.62
  44.9 1.8 %fusion.29 = f32[18,32,8,128]{3,1,2,0:T(8,128)S(1)} fusion(f32[18,32,1,128]{3,1,2,0:T(8,128)S(1)} %collective-permute-done.3, f32[18,32,7,128]{3,1,2,0:T(8,128)S(1)} %slice.250, f32[18,32,8,127]{3,1,2,0:T(8,128)S(1)} %get-tuple-element.15, f32[18,32,8,127]{3,1,2,0:T(8,128)S(1)} %get-tuple-element.14, f32[36,32,8,128]{3,1,2,0:T(8,128)S(1)} %multiply_divide_fusion.2, ...), kind=kLoop, calls=%fused_computation.59 | loop fusion | flops 7667712 | bytes 11768832 | tf_op jit(solution)/shard_map/add | solution.py:41
  46.7 0.6 fusion.6
  47.3 0.1 multiply_add_fusion.2
  47.4 1.4 %multiply_divide_fusion.1 = f32[36,32,8,128]{3,1,2,0:T(8,128)S(1)} fusion(f32[9,32,8,128]{3,1,2,0:T(8,128)S(1)} %get-tuple-element.27, f32[18,32,8,128]{3,1,2,0:T(8,128)S(1)} %fusion.29, f32[9,32,8,128]{3,1,2,0:T(8,128)S(1)} %get-tuple-element.26, f32[32,8,128]{2,0,1:T(8,128)S(1)} %multiply_add_fusion.2, f32[32]{0:T(128)S(1)} %power_multiply_fusion, ...), kind=kLoop, calls=%fused_computation.9 | loop fusion | flops 11796480 | bytes 9719936 | tf_op jit(solution)/shard_map/div | solution.py:58
  48.7 0.9 fusion.55
  49.6 0.3 fusion.56
  50.0 0.2 fusion.39
  50.3 0.2 slice.267
  50.5 4.7 %collective-permute-start.5 = (f32[18,32,1,128]{3,1,2,0:T(8,128)S(1)}, f32[18,32,1,128]{3,1,2,0:T(8,128)S(1)}, u32[]{:S(2)}, u32[]{:S(2)}) collective-permute-start(f32[18,32,1,128]{3,1,2,0:T(8,128)S(1)} %slice.268), channel_id=1, source_target_pairs={{0,15},{1,0},{2,1},{3,2},{4,3},{5,4},{6,5},{7,6},{8,7},{9,8},{10,9... | collective-permute-start | bytes 884744 | tf_op jit(solution)/shard_map/ppermute | solution.py:13
  55.2 0.9 fusion.8
  56.1 2.8 %collective-permute-done.4 = f32[18,32,1,128]{3,1,2,0:T(8,128)S(1)} collective-permute-done((f32[18,32,1,128]{3,1,2,0:T(8,128)S(1)}, f32[18,32,1,128]{3,1,2,0:T(8,128)S(1)}, u32[]{:S(2)}, u32[]{:S(2)}) %collective-permute-start.4) | collective-permute-done | bytes 294944 | tf_op jit(solution)/shard_map/ppermute | solution.py:13
  58.8 1.9 %fusion.34 = f32[18,32,8,128]{3,1,2,0:T(8,128)S(1)} fusion(f32[18,32,7,128]{3,1,2,0:T(8,128)S(1)} %fusion.39, f32[18,32,1,128]{3,1,2,0:T(8,128)S(1)} %collective-permute-done.4, f32[18,32,8,127]{3,1,2,0:T(8,128)S(1)} %get-tuple-element.25, f32[18,32,8,127]{3,1,2,0:T(8,128)S(1)} %get-tuple-element.24, f32[9,32,8,128]{3,1,2,0:T(8,128)S(1)} %get-tuple-element.12, ...), kind=kLoop, calls=%fused_computation.65 | loop fusion | flops 8257536 | bytes 11768832 | tf_op jit(solution)/shard_map/add | solution.py:41
  60.8 0.2 fusion.61
  61.0 1.8 %fusion.38 = f32[18,32,8,128]{3,1,2,0:T(8,128)S(1)} fusion(f32[18,32,1,128]{3,1,2,0:T(8,128)S(1)} %collective-permute-done.5, f32[18,32,7,128]{3,1,2,0:T(8,128)S(1)} %slice.267, f32[18,32,8,127]{3,1,2,0:T(8,128)S(1)} %get-tuple-element.11, f32[18,32,8,127]{3,1,2,0:T(8,128)S(1)} %get-tuple-element.10, f32[36,32,8,128]{3,1,2,0:T(8,128)S(1)} %multiply_divide_fusion.1, ...), kind=kLoop, calls=%fused_computation.70 | loop fusion | flops 7667712 | bytes 11768832 | tf_op jit(solution)/shard_map/add | solution.py:41
  62.8 0.6 fusion.41
  63.4 0.1 multiply_add_fusion.1
  63.5 1.6 %fusion.4 = (f32[36,32,8,128]{3,1,2,0:T(8,128)S(1)}, f32[36,32,8,128]{3,1,2,0:T(8,128)S(1)}) fusion(f32[32]{0:T(128)S(1)} %power_multiply_fusion, f32[36,8,128]{2,1,0:T(8,128)S(1)} %multiply_add_fusion, f32[8,128]{1,0:T(8,128)S(1)} %convert_element_type.3, f32[9,32,8,128]{3,1,2,0:T(8,128)S(1)} %get-tuple-element.23, f32[18,32,8,128]{3,1,2,0:T(8,128)S(1)} %fusion.38, ...), kind=kLoop, calls=%fused_computation.12 | loop fusion | flops 12976128 | bytes 14438528 | tf_op jit(solution)/shard_map/mul | solution.py:58
  65.0 2.4 %fusion.42 = f32[2,8,128]{2,0,1:T(2,128)S(1)} fusion(f32[2,36,32,1]{2,0,1,3:T(2,128)S(1)} %copy.44, f32[36,32,8,128]{3,1,2,0:T(8,128)S(1)} %get-tuple-element.8), kind=kOutput, calls=%fused_computation.76 | convolution fusion | flops 28311552 | bytes 4736000 | tf_op jit(solution)/shard_map/cij,ijxy->cxy/dot_general | solution.py:62
  67.4 2.4 %fusion.45 = f32[2,8,128]{2,0,1:T(2,128)S(1)} fusion(f32[2,36,32,1]{2,0,1,3:T(2,128)S(1)} %copy.44, f32[36,32,8,128]{3,1,2,0:T(8,128)S(1)} %get-tuple-element.9), kind=kOutput, calls=%fused_computation.77 | convolution fusion | flops 28311552 | bytes 4736000 | tf_op jit(solution)/shard_map/cij,ijxy->cxy/dot_general | solution.py:63
  69.9 0.2 copy.39
  70.0 0.8 gather_fusion
  70.8 0.1 copy.40
  70.9 0.8 stack.5
  71.6 4.4 %all-to-all-start = ((f32[16,4,128,8]{2,3,1,0:T(8,128)}), f32[16,4,128,8]{2,3,1,0:T(8,128)S(1)}, u32[]{:S(2)}, u32[]{:S(2)}) async-start(f32[16,4,128,8]{2,3,1,0:T(8,128)} %stack.5), calls=%async_computation | async-start | bytes 524288 | tf_op jit(solution)/shard_map/all_to_all | solution.py:90
  76.1 8.9 %copy.42 = f32[36,32,8,128]{3,2,1,0:T(8,128)} copy(f32[36,32,8,128]{3,1,2,0:T(8,128)} %copy-done) | data formatting | bytes 9437184
  85.0 1.1 %all-to-all-done = f32[16,4,128,8]{2,3,1,0:T(8,128)S(1)} async-done(((f32[16,4,128,8]{2,3,1,0:T(8,128)}), f32[16,4,128,8]{2,3,1,0:T(8,128)S(1)}, u32[]{:S(2)}, u32[]{:S(2)}) %all-to-all-start) | async-done | bytes 262176 | tf_op jit(solution)/shard_map/all_to_all | solution.py:90
  86.1 0.1 constant_dynamic-slice_fusion
  86.3 0.7 copy.43
  (46 shorter events, 0.5 us)
Async XLA Ops:
  2.4 2.4 %copy-start.1 = (f32[36,32,8,128]{3,2,1,0:T(8,128)S(1)}, f32[36,32,8,128]{3,2,1,0:T(8,128)}, u32[]{:S(2)}) copy-start(f32[36,32,8,128]{3,2,1,0:T(8,128)} %param.4) | copy-start | bytes 14155780
  3.6 18.8 %collective-permute-start = (f32[18,32,1,128]{3,1,2,0:T(8,128)}, f32[18,32,1,128]{3,1,2,0:T(8,128)S(1)}, u32[]{:S(2)}, u32[]{:S(2)}) collective-permute-start(f32[18,32,1,128]{3,1,2,0:T(8,128)} %slice.228), channel_id=1, source_target_pairs={{0,1},{1,2},{2,3},{3,4},{4,5},{5,6},{6,7},{7,8},{8,9},{9,10},{10,1... | collective-permute-start | bytes 884744 | tf_op jit(solution)/shard_map/ppermute | solution.py:13
  5.1 21.7 %collective-permute-start.1 = (f32[18,32,1,128]{3,1,2,0:T(8,128)S(1)}, f32[18,32,1,128]{3,1,2,0:T(8,128)S(1)}, u32[]{:S(2)}, u32[]{:S(2)}) collective-permute-start(f32[18,32,1,128]{3,1,2,0:T(8,128)S(1)} %bitcast.24), channel_id=1, source_target_pairs={{0,15},{1,0},{2,1},{3,2},{4,3},{5,4},{6,5},{7,6},{8,7},{9,8},{10,9... | collective-permute-start | bytes 884744 | tf_op jit(solution)/shard_map/ppermute | solution.py:13
  20.3 1.7 %copy-start.6 = (s32[8,128]{1,0:T(8,128)S(1)}, s32[8,128]{1,0:T(8,128)}, u32[]{:S(2)}) copy-start(s32[8,128]{1,0:T(8,128)} %param.6) | copy-start | bytes 12292
  20.3 1.7 %copy-start.5 = (f32[2,8,128]{2,1,0:T(8,128)S(1)}, f32[2,8,128]{2,1,0:T(8,128)}, u32[]{:S(2)}) copy-start(f32[2,8,128]{2,1,0:T(8,128)} %param.5) | copy-start | bytes 24580
  20.3 1.9 %copy-start.7 = (s32[128]{0:T(128)S(1)}, s32[128]{0:T(128)}, u32[]{:S(2)}) copy-start(s32[128]{0:T(128)} %param.7) | copy-start | bytes 1540
  22.4 4.3 %copy-start.3 = (f32[18,32,8,127]{3,1,2,0:T(8,128)S(1)}, f32[18,32,8,127]{3,1,2,0:T(8,128)}, u32[]{:S(2)}) copy-start(f32[18,32,8,127]{3,1,2,0:T(8,128)} %copy.62) | copy-start | bytes 7022596
  22.4 4.3 %copy-start.4 = (f32[18,32,7,128]{3,1,2,0:T(8,128)S(1)}, f32[18,32,7,128]{3,1,2,0:T(8,128)}, u32[]{:S(2)}) copy-start(f32[18,32,7,128]{3,1,2,0:T(8,128)} %copy.59) | copy-start | bytes 6193156
  26.4 1.7 %slice-start = ((f32[36,32,8,128]{3,2,1,0:T(8,128)}), f32[18,32,8,128]{3,2,1,0:T(8,128)S(1)}, s32[]{:S(2)}) async-start(f32[36,32,8,128]{3,2,1,0:T(8,128)} %param.4), calls=%async_computation.1 | async-start | bytes 4718592 | tf_op jit(solution)/shard_map/slice | solution.py:78
  26.4 2.4 %copy-start.2 = (f32[18,32,8,127]{3,1,2,0:T(8,128)S(1)}, f32[18,32,8,127]{3,1,2,0:T(8,128)}, u32[]{:S(2)}) copy-start(f32[18,32,8,127]{3,1,2,0:T(8,128)} %copy.61) | copy-start | bytes 7022596
  33.8 8.9 %collective-permute-start.2 = (f32[18,32,1,128]{3,1,2,0:T(8,128)S(1)}, f32[18,32,1,128]{3,1,2,0:T(8,128)S(1)}, u32[]{:S(2)}, u32[]{:S(2)}) collective-permute-start(f32[18,32,1,128]{3,1,2,0:T(8,128)S(1)} %fusion.49), channel_id=1, source_target_pairs={{0,1},{1,2},{2,3},{3,4},{4,5},{5,6},{6,7},{7,8},{8,9},{9,10},{10,1... | collective-permute-start | bytes 884744 | tf_op jit(solution)/shard_map/ppermute | solution.py:13
  34.4 10.5 %collective-permute-start.3 = (f32[18,32,1,128]{3,1,2,0:T(8,128)S(1)}, f32[18,32,1,128]{3,1,2,0:T(8,128)S(1)}, u32[]{:S(2)}, u32[]{:S(2)}) collective-permute-start(f32[18,32,1,128]{3,1,2,0:T(8,128)S(1)} %slice.251), channel_id=1, source_target_pairs={{0,15},{1,0},{2,1},{3,2},{4,3},{5,4},{6,5},{7,6},{8,7},{9,8},{10,9... | collective-permute-start | bytes 884744 | tf_op jit(solution)/shard_map/ppermute | solution.py:13
  49.9 8.9 %collective-permute-start.4 = (f32[18,32,1,128]{3,1,2,0:T(8,128)S(1)}, f32[18,32,1,128]{3,1,2,0:T(8,128)S(1)}, u32[]{:S(2)}, u32[]{:S(2)}) collective-permute-start(f32[18,32,1,128]{3,1,2,0:T(8,128)S(1)} %fusion.48), channel_id=1, source_target_pairs={{0,1},{1,2},{2,3},{3,4},{4,5},{5,6},{6,7},{7,8},{8,9},{9,10},{10,1... | collective-permute-start | bytes 884744 | tf_op jit(solution)/shard_map/ppermute | solution.py:13
  50.5 10.5 %collective-permute-start.5 = (f32[18,32,1,128]{3,1,2,0:T(8,128)S(1)}, f32[18,32,1,128]{3,1,2,0:T(8,128)S(1)}, u32[]{:S(2)}, u32[]{:S(2)}) collective-permute-start(f32[18,32,1,128]{3,1,2,0:T(8,128)S(1)} %slice.268), channel_id=1, source_target_pairs={{0,15},{1,0},{2,1},{3,2},{4,3},{5,4},{6,5},{7,6},{8,7},{9,8},{10,9... | collective-permute-start | bytes 884744 | tf_op jit(solution)/shard_map/ppermute | solution.py:13
  65.0 2.4 %copy-start = (f32[36,32,8,128]{3,1,2,0:T(8,128)}, f32[36,32,8,128]{3,1,2,0:T(8,128)S(1)}, u32[]{:S(2)}) copy-start(f32[36,32,8,128]{3,1,2,0:T(8,128)S(1)} %get-tuple-element.9) | copy-start | bytes 14155780
  71.6 14.5 %all-to-all-start = ((f32[16,4,128,8]{2,3,1,0:T(8,128)}), f32[16,4,128,8]{2,3,1,0:T(8,128)S(1)}, u32[]{:S(2)}, u32[]{:S(2)}) async-start(f32[16,4,128,8]{2,3,1,0:T(8,128)} %stack.5), calls=%async_computation | async-start | bytes 524288 | tf_op jit(solution)/shard_map/all_to_all | solution.py:90
